TPU v7x, 32 devices: a whole 2x2x4 slice. The times are simulated.
32 devices in a mesh: col: 8 (over z, y), row: 4 (over x, core).
Axes of the slice: x: 2, y: 2, z: 4, core: 2. Of those that a mesh axis runs over, the one named last changes fastest.
Arguments:
- right_side: float32 [8192, 256], P(('row', 'col')), may hold values from -6 to 6
- prior_solution: bfloat16 [16384, 256], P('col'), may hold values from -6 to 6
- factor_codes: bfloat16 [8192, 16384], P('row', 'col'), may hold values from -0.046875 to 0.046875
- block_scale: float32 [4, 64], P('row', 'col'), may hold values from 0.3 to 3
- diag_inverse: bfloat16 [4, 2048, 2048], P('row', 'col'), may hold values from -0.125 to 0.125
- inner_factor: bfloat16 [4, 4, 2048, 2048], P('row', None, 'col'), may hold values from -0.125 to 0.125
Outputs:
- solved: float32 [8192, 256], P(('row', 'col'))
All inputs are finite; a program needn't handle non-finite values.
Results may differ from a plain program's by a relative error of at most 0.0095.
Values may be sent and summed in bfloat16 or wider, within the bound.
No kernel may reach another device: no remote copies, remote signals or barrier semaphores. Data moves between devices by JAX's collectives and lax.ppermute only.
A program may use at most 64 MiB of HBM per device.

v0:
```python
import jax
import jax.numpy as jnp
from jax import lax
from jax.sharding import PartitionSpec as P


def from_root(value, axis, source):
    kept = jnp.where(lax.axis_index(axis) == source, value, 0).astype(value.dtype)
    return lax.psum(kept, axis)


def local(right_side, prior_solution, factor_codes, block_scale, diag_inverse, inner_factor):
    rows_each = right_side.shape[0]
    panel_rows = factor_codes.shape[0]
    blocks_here = block_scale.shape[1]
    block_cols = factor_codes.shape[1] // blocks_here
    columns_out = right_side.shape[1]
    summed = jnp.zeros((panel_rows, columns_out), jnp.float32)
    for column_block in range(blocks_here):
        coded = lax.dynamic_slice(
            factor_codes, (0, column_block * block_cols), (panel_rows, block_cols)
        )
        earlier = prior_solution[column_block * block_cols : (column_block + 1) * block_cols]
        summed = summed + block_scale[0, column_block] * jnp.dot(
            coded, earlier, preferred_element_type=jnp.float32
        )
    prior_rows = lax.psum_scatter(summed, "col", scatter_dimension=0, tiled=True)
    rhs = right_side - prior_rows
    row_place = lax.axis_index("row")
    solved = jnp.zeros((rows_each, columns_out), jnp.float32)
    inverse_rows = diag_inverse[0]
    panel_count = lax.axis_size("row")
    for section in range(panel_count):
        rounded = rhs.astype(jnp.bfloat16)
        current = jnp.dot(
            inverse_rows,
            lax.all_gather(rounded, "col", axis=0, tiled=True),
            preferred_element_type=jnp.float32,
        )
        solved = jnp.where(row_place == section, current, solved)
        if section + 1 < panel_count:
            sending = current.astype(jnp.bfloat16)
            coupling = inner_factor[0, section]
            whole_panel = lax.all_gather(sending, "col", axis=0, tiled=True)
            copied = from_root(whole_panel, "row", section)
            update = jnp.dot(coupling, copied, preferred_element_type=jnp.float32)
            rhs = rhs - jnp.where(row_place > section, update, 0.0)
    return solved


def solution(mesh):
    return jax.shard_map(
        local,
        mesh=mesh,
        in_specs=(
            P(("row", "col"), None),
            P("col", None),
            P("row", "col"),
            P("row", "col"),
            P("row", "col", None),
            P("row", None, "col", None),
        ),
        out_specs=P(("row", "col"), None),
        check_vma=False,
    )
```

profile of v0, /device:TPU:0, one launch (start us, length us, event | category | flops | bytes accessed | tf_op | source)
XLA Modules:
  0.0 509.4 jit_solution(15707440207164434849)
XLA Ops:
  6.5 1.6 fusion.45
  8.2 2.5 convolution_multiply_fusion.7
  10.7 2.5 fusion.6
  13.3 2.0 fusion.5
  15.3 1.1 fusion.4
  16.4 1.1 fusion.3
  17.5 1.1 fusion.2
  18.6 1.0 fusion.1
  19.6 2.4 fusion
  22.0 0.0 reduce-scatter.2.cloned.1.call-update
  22.0 0.0 all-gather.8.cloned.1.call-start
  22.1 71.2 %reduce-scatter.2.cloned.1.call-done = f32[256,256]{1,0:T(8,128)} async-done(((f32[2048,256]{1,0:T(8,128)}), f32[256,256]{1,0:T(8,128)}) %reduce-scatter.2.cloned.1.call-update) | async-done | bytes 262160 | tf_op jit(solution)/shard_map/reduce_scatter | solution.py:27
  93.2 1.6 fusion.44
  94.9 0.0 all-gather.10.cloned.1.call-start
  95.0 39.7 %all-gather.8.cloned.1.call-done = bf16[2048,256]{1,0:T(8,128)(2,1)} async-done(((bf16[256,256]{1,0:T(8,128)(2,1)}), bf16[2048,256]{1,0:T(8,128)(2,1)}) %all-gather.8.cloned.1.call-update) | async-done | bytes 1048592 | tf_op jit(solution)/shard_map/all_gather | solution.py:37
  134.7 1.7 fusion.23
  136.4 0.7 convert_bitcast_fusion.2
  137.1 0.0 all-reduce.4.cloned.1.call-start
  137.2 38.2 %all-gather.10.cloned.1.call-done = bf16[2048,256]{0,1:T(8,128)(2,1)} async-done(((bf16[256,256]{0,1:T(8,128)(2,1)}), bf16[2048,256]{0,1:T(8,128)(2,1)}) %all-gather.10.cloned.1.call-update) | async-done | bytes 1048592 | tf_op jit(solution)/shard_map/all_gather | solution.py:44
  175.4 2.3 broadcast_select_fusion.2
  177.7 0.0 all-gather.12.cloned.1.call-start
  177.7 35.2 %all-reduce.4.cloned.1.call-done = bf16[2048,256]{0,1:T(8,128)(2,1)} async-done(((bf16[2048,256]{0,1:T(8,128)(2,1)}), bf16[2048,256]{0,1:T(8,128)(2,1)}) %all-reduce.4.cloned.1.call-update) | async-done | bytes 1048592 | tf_op jit(solution)/shard_map/psum | solution.py:9
  212.9 2.7 fusion.46
  215.6 0.0 all-gather.14.cloned.1.call-start
  215.7 40.9 %all-gather.12.cloned.1.call-done = bf16[2048,256]{1,0:T(8,128)(2,1)} async-done(((bf16[256,256]{1,0:T(8,128)(2,1)}), bf16[2048,256]{1,0:T(8,128)(2,1)}) %all-gather.12.cloned.1.call-update) | async-done | bytes 1048592 | tf_op jit(solution)/shard_map/all_gather | solution.py:37
  256.5 1.7 fusion.21
  258.2 0.7 convert_bitcast_fusion.1
  258.9 0.0 all-reduce.6.cloned.1.call-start
  259.0 38.2 %all-gather.14.cloned.1.call-done = bf16[2048,256]{0,1:T(8,128)(2,1)} async-done(((bf16[256,256]{0,1:T(8,128)(2,1)}), bf16[2048,256]{0,1:T(8,128)(2,1)}) %all-gather.14.cloned.1.call-update) | async-done | bytes 1048592 | tf_op jit(solution)/shard_map/all_gather | solution.py:44
  297.2 1.1 broadcast_select_fusion.1
  298.3 0.0 all-gather.16.cloned.1.call-start
  298.3 36.5 %all-reduce.6.cloned.1.call-done = bf16[2048,256]{0,1:T(8,128)(2,1)} async-done(((bf16[2048,256]{0,1:T(8,128)(2,1)}), bf16[2048,256]{0,1:T(8,128)(2,1)}) %all-reduce.6.cloned.1.call-update) | async-done | bytes 1048592 | tf_op jit(solution)/shard_map/psum | solution.py:9
  334.9 2.7 fusion.47
  337.6 0.0 all-gather.18.cloned.1.call-start
  337.6 40.9 %all-gather.16.cloned.1.call-done = bf16[2048,256]{1,0:T(8,128)(2,1)} async-done(((bf16[256,256]{1,0:T(8,128)(2,1)}), bf16[2048,256]{1,0:T(8,128)(2,1)}) %all-gather.16.cloned.1.call-update) | async-done | bytes 1048592 | tf_op jit(solution)/shard_map/all_gather | solution.py:37
  378.5 1.7 fusion.19
  380.2 0.7 convert_bitcast_fusion
  380.9 0.0 all-reduce.8.cloned.1.call-start
  381.0 38.2 %all-gather.18.cloned.1.call-done = bf16[2048,256]{0,1:T(8,128)(2,1)} async-done(((bf16[256,256]{0,1:T(8,128)(2,1)}), bf16[2048,256]{0,1:T(8,128)(2,1)}) %all-gather.18.cloned.1.call-update) | async-done | bytes 1048592 | tf_op jit(solution)/shard_map/all_gather | solution.py:44
  419.2 1.1 broadcast_select_fusion
  420.2 0.0 all-gather.20.cloned.1.call-start
  420.3 36.6 %all-reduce.8.cloned.1.call-done = bf16[2048,256]{0,1:T(8,128)(2,1)} async-done(((bf16[2048,256]{0,1:T(8,128)(2,1)}), bf16[2048,256]{0,1:T(8,128)(2,1)}) %all-reduce.8.cloned.1.call-update) | async-done | bytes 1048592 | tf_op jit(solution)/shard_map/psum | solution.py:9
  456.9 2.7 fusion.14
  459.6 0.1 copy.9
  459.8 0.1 copy.10
  459.9 0.1 copy.11
  460.0 40.5 %all-gather.20.cloned.1.call-done = bf16[2048,256]{1,0:T(8,128)(2,1)} async-done(((bf16[256,256]{1,0:T(8,128)(2,1)}), bf16[2048,256]{1,0:T(8,128)(2,1)}) %all-gather.20.cloned.1.call-update) | async-done | bytes 1048592 | tf_op jit(solution)/shard_map/all_gather | solution.py:37
  500.5 2.4 fusion.7
  (19 shorter events, 0.2 us)
Async XLA Ops:
  6.5 128.2 %copy-start = (bf16[1,256,2048]{2,1,0:T(8,128)(2,1)S(1)}, bf16[1,256,2048]{2,1,0:T(8,128)(2,1)}, u32[]{:S(2)}) copy-start(bf16[1,256,2048]{2,1,0:T(8,128)(2,1)} %param.10) | copy-start | bytes 3145732
  6.5 86.7 %reduce-scatter.2.cloned.1.call-start = ((), (), s32[]{:S(2)}) async-start(), calls=%async_computation.1 | async-start | bytes 2359296 | tf_op jit(solution)/shard_map/reduce_scatter | solution.py:27
  8.2 5.1 copy-start.1
  13.3 2.0 copy-start.2
  22.0 71.2 %copy-start.3 = (f32[256,256]{1,0:T(8,128)S(1)}, f32[256,256]{1,0:T(8,128)}, u32[]{:S(2)}) copy-start(f32[256,256]{1,0:T(8,128)} %param.6) | copy-start | bytes 786436
  22.0 112.7 %all-gather.8.cloned.1.call-start = ((), (), s32[]{:S(2)}) async-start(), calls=%async_computation.2 | async-start | bytes 1179648 | tf_op jit(solution)/shard_map/all_gather | solution.py:37
  94.9 80.5 %all-gather.10.cloned.1.call-start = ((), (), s32[]{:S(2)}) async-start(), calls=%async_computation.3 | async-start | bytes 1179648 | tf_op jit(solution)/shard_map/all_gather | solution.py:44
  137.1 75.8 %all-reduce.4.cloned.1.call-start = ((), (), s32[]{:S(2)}) async-start(), calls=%async_computation.4 | async-start | bytes 2097152 | tf_op jit(solution)/shard_map/psum | solution.py:9
  177.7 78.9 %all-gather.12.cloned.1.call-start = ((), (), s32[]{:S(2)}) async-start(), calls=%async_computation.5 | async-start | bytes 1179648 | tf_op jit(solution)/shard_map/all_gather | solution.py:37
  215.6 81.6 %all-gather.14.cloned.1.call-start = ((), (), s32[]{:S(2)}) async-start(), calls=%async_computation.6 | async-start | bytes 1179648 | tf_op jit(solution)/shard_map/all_gather | solution.py:44
  258.9 75.9 %all-reduce.6.cloned.1.call-start = ((), (), s32[]{:S(2)}) async-start(), calls=%async_computation.7 | async-start | bytes 2097152 | tf_op jit(solution)/shard_map/psum | solution.py:9
  298.3 80.2 %all-gather.16.cloned.1.call-start = ((), (), s32[]{:S(2)}) async-start(), calls=%async_computation.8 | async-start | bytes 1179648 | tf_op jit(solution)/shard_map/all_gather | solution.py:37
  337.6 81.6 %all-gather.18.cloned.1.call-start = ((), (), s32[]{:S(2)}) async-start(), calls=%async_computation.9 | async-start | bytes 1179648 | tf_op jit(solution)/shard_map/all_gather | solution.py:44
  380.9 76.0 %all-reduce.8.cloned.1.call-start = ((), (), s32[]{:S(2)}) async-start(), calls=%async_computation.10 | async-start | bytes 2097152 | tf_op jit(solution)/shard_map/psum | solution.py:9
  420.2 80.3 %all-gather.20.cloned.1.call-start = ((), (), s32[]{:S(2)}) async-start(), calls=%async_computation.11 | async-start | bytes 1179648 | tf_op jit(solution)/shard_map/all_gather | solution.py:37
Sparse Core Ops, SparseCore 0:
  22.2 71.0 reduce-scatter.1
  95.4 39.2 all-gather.7
  137.2 38.0 all-gather.9
  177.8 35.0 all-reduce.3
  215.8 40.7 all-gather.11
  259.1 38.0 all-gather.13
  299.6 35.2 all-reduce.5
  337.7 40.7 all-gather.15
  381.0 38.0 all-gather.17
  421.4 35.4 all-reduce.7
  459.7 40.7 all-gather.19
where the time goes:
time: 510 us; the launch traced here: 509 us
  waiting for transfers between devices  456 us (89%)
  matrix products  29.3 us (6%)
  between operations  13.4 us (3%)
  other arithmetic  8.06 us (2%)
    all_gather x4, waiting for transfers between devices, local(): lax.all_gather(rounded, 'col', axis=0, tiled=True)  162 us
    all_gather x3, waiting for transfers between devices, local(): whole_panel = lax.all_gather(sending, 'col', axis=0, tiled=True)  115 us
    psum x3, waiting for transfers between devices, from_root(): return lax.psum(kept, axis)  108 us
    reduce_scatter x1, waiting for transfers between devices, local(): lax.psum_scatter(summed, 'col', scatter_dimension=0, tiled=True)  71.2 us
    dot_general x8, matrix products, local(): jnp.dot(coded, earlier, preferred_element_type=jnp.float32)  13.7 us
  transfers between devices with their start and end apart: 11, of which 11 were waited for; matrix products, arithmetic and copies ran while one was open for 0% of the time, Pallas kernels for 0%

commit v1 on v0

--- a/solution.py
+++ b/solution.py
@@ -41,7 +41,8 @@
         if section + 1 < panel_count:
             sending = current.astype(jnp.bfloat16)
             coupling = inner_factor[0, section]
-            whole_panel = lax.all_gather(sending, "col", axis=0, tiled=True)
+            sent = jnp.stack([sending] * lax.axis_size("col"))
+            whole_panel = jnp.concatenate(lax.all_to_all(sent, "col", 0, 0), axis=0)
             copied = from_root(whole_panel, "row", section)
             update = jnp.dot(coupling, copied, preferred_element_type=jnp.float32)
             rhs = rhs - jnp.where(row_place > section, update, 0.0)

time: 510 us -> 477 us (0.935)
  waiting for transfers between devices: 456 us -> 412 us
  starting transfers between devices: 0.42 us -> 11 us
    all_gather x3 -> x0, waiting for transfers between devices: 115 us -> none  [local(): whole_panel = lax.all_gather(sending, 'col', axis=0, tiled=True)]
    all_to_all x0 -> x3, waiting for transfers between devices: none -> 73.2 us  [local(): whole_panel = jnp.concatenate(lax.all_to_all(sent, 'col', 0, 0), axis=0)]
    all_to_all x0 -> x3, starting transfers between devices: none -> 10.7 us  [local(): whole_panel = jnp.concatenate(lax.all_to_all(sent, 'col', 0, 0), axis=0)]
where the time goes in v1:
time: 477 us; the launch traced here: 476 us
  waiting for transfers between devices  412 us (86%)
  matrix products  29.2 us (6%)
  between operations  13.7 us (3%)
  starting transfers between devices  11 us (2%)
  local copies, waits for them, and re-layouts  5.58 us (1%)
  other arithmetic  4.8 us (1%)
    all_gather x4, waiting for transfers between devices, local(): lax.all_gather(rounded, 'col', axis=0, tiled=True)  162 us
    psum x3, waiting for transfers between devices, from_root(): return lax.psum(kept, axis)  106 us
    all_to_all x3, waiting for transfers between devices, local(): whole_panel = jnp.concatenate(lax.all_to_all(sent, 'col', 0, 0), axis=0)  73.2 us
    reduce_scatter x1, waiting for transfers between devices, local(): lax.psum_scatter(summed, 'col', scatter_dimension=0, tiled=True)  71.2 us
    dot_general x8, matrix products, local(): jnp.dot(coded, earlier, preferred_element_type=jnp.float32)  13.8 us
    all_to_all x3, starting transfers between devices, local(): whole_panel = jnp.concatenate(lax.all_to_all(sent, 'col', 0, 0), axis=0)  10.7 us
  transfers between devices with their start and end apart: 11, of which 11 were waited for; matrix products, arithmetic and copies ran while one was open for 0% of the time, Pallas kernels for 0%

profile of v1, /device:TPU:0, one launch (start us, length us, event | category | flops | bytes accessed | tf_op | source)
XLA Modules:
  0.0 476.5 jit_solution(8811132779592236687)
XLA Ops:
  6.5 1.6 fusion.45
  8.2 2.6 convolution_multiply_fusion.7
  10.8 2.4 fusion.6
  13.2 2.1 fusion.5
  15.3 1.1 fusion.4
  16.5 1.1 fusion.3
  17.6 1.0 fusion.2
  18.6 1.0 fusion.1
  19.6 2.4 fusion
  22.1 0.0 all-gather.5.cloned.1.call-start
  22.1 71.2 %reduce-scatter.2.cloned.1.call-done = f32[256,256]{1,0:T(8,128)} async-done(((f32[2048,256]{1,0:T(8,128)}), f32[256,256]{1,0:T(8,128)}) %reduce-scatter.2.cloned.1.call-update) | async-done | bytes 262160 | tf_op jit(solution)/shard_map/reduce_scatter | solution.py:27
  93.3 1.6 fusion.44
  95.0 39.7 %all-gather.5.cloned.1.call-done = bf16[2048,256]{1,0:T(8,128)(2,1)} async-done(((bf16[256,256]{1,0:T(8,128)(2,1)}), bf16[2048,256]{1,0:T(8,128)(2,1)}) %all-gather.5.cloned.1.call-update) | async-done | bytes 1048592 | tf_op jit(solution)/shard_map/all_gather | solution.py:37
  134.7 1.7 fusion.23
  136.5 0.1 copy.7
  136.6 1.1 stack.6
  137.7 3.6 all-to-all-start
  141.2 0.0 all-reduce.4.cloned.1.call-start
  141.3 24.4 %all-to-all-done = bf16[8,256,256]{2,1,0:T(8,128)(2,1)S(1)} async-done(((bf16[8,256,256]{2,1,0:T(8,128)(2,1)}), bf16[8,256,256]{2,1,0:T(8,128)(2,1)S(1)}, u32[]{:S(2)}, u32[]{:S(2)}) %all-to-all-start) | async-done | bytes 1048608 | tf_op jit(solution)/shard_map/all_to_all | solution.py:45
  165.7 1.0 broadcast_select_fusion.2
  166.7 0.0 all-gather.7.cloned.1.call-start
  166.8 35.2 %all-reduce.4.cloned.1.call-done = bf16[2048,256]{1,0:T(8,128)(2,1)} async-done(((bf16[2048,256]{1,0:T(8,128)(2,1)}), bf16[2048,256]{1,0:T(8,128)(2,1)}) %all-reduce.4.cloned.1.call-update) | async-done | bytes 1048592 | tf_op jit(solution)/shard_map/psum | solution.py:9
  202.0 2.6 fusion.46
  204.7 40.9 %all-gather.7.cloned.1.call-done = bf16[2048,256]{1,0:T(8,128)(2,1)} async-done(((bf16[256,256]{1,0:T(8,128)(2,1)}), bf16[2048,256]{1,0:T(8,128)(2,1)}) %all-gather.7.cloned.1.call-update) | async-done | bytes 1048592 | tf_op jit(solution)/shard_map/all_gather | solution.py:37
  245.6 1.7 fusion.21
  247.3 0.1 copy.9
  247.4 1.1 stack.7
  248.5 3.6 all-to-all-start.1
  252.1 0.0 all-reduce.6.cloned.1.call-start
  252.1 24.4 %all-to-all-done.1 = bf16[8,256,256]{2,1,0:T(8,128)(2,1)S(1)} async-done(((bf16[8,256,256]{2,1,0:T(8,128)(2,1)}), bf16[8,256,256]{2,1,0:T(8,128)(2,1)S(1)}, u32[]{:S(2)}, u32[]{:S(2)}) %all-to-all-start.1) | async-done | bytes 1048608 | tf_op jit(solution)/shard_map/all_to_all | solution.py:45
  276.5 1.0 broadcast_select_fusion.1
  277.6 0.0 all-gather.9.cloned.1.call-start
  277.6 35.2 %all-reduce.6.cloned.1.call-done = bf16[2048,256]{1,0:T(8,128)(2,1)} async-done(((bf16[2048,256]{1,0:T(8,128)(2,1)}), bf16[2048,256]{1,0:T(8,128)(2,1)}) %all-reduce.6.cloned.1.call-update) | async-done | bytes 1048592 | tf_op jit(solution)/shard_map/psum | solution.py:9
  312.9 2.6 fusion.47
  315.5 40.9 %all-gather.9.cloned.1.call-done = bf16[2048,256]{1,0:T(8,128)(2,1)} async-done(((bf16[256,256]{1,0:T(8,128)(2,1)}), bf16[2048,256]{1,0:T(8,128)(2,1)}) %all-gather.9.cloned.1.call-update) | async-done | bytes 1048592 | tf_op jit(solution)/shard_map/all_gather | solution.py:37
  356.4 1.7 fusion.19
  358.2 0.1 copy.11
  358.3 1.1 stack.8
  359.4 3.6 all-to-all-start.2
  363.0 24.4 %all-to-all-done.2 = bf16[8,256,256]{2,1,0:T(8,128)(2,1)S(1)} async-done(((bf16[8,256,256]{2,1,0:T(8,128)(2,1)}), bf16[8,256,256]{2,1,0:T(8,128)(2,1)S(1)}, u32[]{:S(2)}, u32[]{:S(2)}) %all-to-all-start.2) | async-done | bytes 1048608 | tf_op jit(solution)/shard_map/all_to_all | solution.py:45
  387.4 1.0 broadcast_select_fusion
  388.5 35.2 %all-reduce.8.cloned.1.call-done = bf16[2048,256]{1,0:T(8,128)(2,1)} async-done(((bf16[2048,256]{1,0:T(8,128)(2,1)}), bf16[2048,256]{1,0:T(8,128)(2,1)}) %all-reduce.8.cloned.1.call-update) | async-done | bytes 1048592 | tf_op jit(solution)/shard_map/psum | solution.py:9
  423.7 2.6 fusion.14
  426.4 0.1 copy.12
  426.5 0.1 copy.13
  426.6 0.1 copy.14
  426.8 40.5 %all-gather.11.cloned.1.call-done = bf16[2048,256]{1,0:T(8,128)(2,1)} async-done(((bf16[256,256]{1,0:T(8,128)(2,1)}), bf16[2048,256]{1,0:T(8,128)(2,1)}) %all-gather.11.cloned.1.call-update) | async-done | bytes 1048592 | tf_op jit(solution)/shard_map/all_gather | solution.py:37
  467.3 2.4 fusion.7
  (22 shorter events, 0.3 us)
Async XLA Ops:
  6.5 128.2 %copy-start = (bf16[1,256,2048]{2,1,0:T(8,128)(2,1)S(1)}, bf16[1,256,2048]{2,1,0:T(8,128)(2,1)}, u32[]{:S(2)}) copy-start(bf16[1,256,2048]{2,1,0:T(8,128)(2,1)} %param.10) | copy-start | bytes 3145732
  6.5 86.8 %reduce-scatter.2.cloned.1.call-start = ((), (), s32[]{:S(2)}) async-start(), calls=%async_computation.4 | async-start | bytes 2359296 | tf_op jit(solution)/shard_map/reduce_scatter | solution.py:27
  8.2 5.1 %copy-start.1 = (bf16[2048,2048]{1,0:T(8,128)(2,1)S(1)}, bf16[2048,2048]{1,0:T(8,128)(2,1)}, u32[]{:S(2)}) copy-start(bf16[2048,2048]{1,0:T(8,128)(2,1)} %param.8) | copy-start | bytes 25165828
  13.2 2.1 copy-start.2
  22.0 71.3 %copy-start.3 = (f32[256,256]{1,0:T(8,128)S(1)}, f32[256,256]{1,0:T(8,128)}, u32[]{:S(2)}) copy-start(f32[256,256]{1,0:T(8,128)} %param.6) | copy-start | bytes 786436
  22.1 112.7 %all-gather.5.cloned.1.call-start = ((), (), s32[]{:S(2)}) async-start(), calls=%async_computation.5 | async-start | bytes 1179648 | tf_op jit(solution)/shard_map/all_gather | solution.py:37
  137.7 28.0 %all-to-all-start = ((bf16[8,256,256]{2,1,0:T(8,128)(2,1)}), bf16[8,256,256]{2,1,0:T(8,128)(2,1)S(1)}, u32[]{:S(2)}, u32[]{:S(2)}) async-start(bf16[8,256,256]{2,1,0:T(8,128)(2,1)} %stack.6), calls=%async_computation.1 | async-start | bytes 2097152 | tf_op jit(solution)/shard_map/all_to_all | solution.py:45
  141.2 60.8 %all-reduce.4.cloned.1.call-start = ((), (), s32[]{:S(2)}) async-start(), calls=%async_computation.6 | async-start | bytes 2097152 | tf_op jit(solution)/shard_map/psum | solution.py:9
  166.7 78.8 %all-gather.7.cloned.1.call-start = ((), (), s32[]{:S(2)}) async-start(), calls=%async_computation.7 | async-start | bytes 1179648 | tf_op jit(solution)/shard_map/all_gather | solution.py:37
  248.5 28.0 %all-to-all-start.1 = ((bf16[8,256,256]{2,1,0:T(8,128)(2,1)}), bf16[8,256,256]{2,1,0:T(8,128)(2,1)S(1)}, u32[]{:S(2)}, u32[]{:S(2)}) async-start(bf16[8,256,256]{2,1,0:T(8,128)(2,1)} %stack.7), calls=%async_computation.2 | async-start | bytes 2097152 | tf_op jit(solution)/shard_map/all_to_all | solution.py:45
  252.1 60.8 %all-reduce.6.cloned.1.call-start = ((), (), s32[]{:S(2)}) async-start(), calls=%async_computation.8 | async-start | bytes 2097152 | tf_op jit(solution)/shard_map/psum | solution.py:9
  277.6 78.8 %all-gather.9.cloned.1.call-start = ((), (), s32[]{:S(2)}) async-start(), calls=%async_computation.9 | async-start | bytes 1179648 | tf_op jit(solution)/shard_map/all_gather | solution.py:37
  359.4 28.0 %all-to-all-start.2 = ((bf16[8,256,256]{2,1,0:T(8,128)(2,1)}), bf16[8,256,256]{2,1,0:T(8,128)(2,1)S(1)}, u32[]{:S(2)}, u32[]{:S(2)}) async-start(bf16[8,256,256]{2,1,0:T(8,128)(2,1)} %stack.8), calls=%async_computation.3 | async-start | bytes 2097152 | tf_op jit(solution)/shard_map/all_to_all | solution.py:45
  362.9 60.8 %all-reduce.8.cloned.1.call-start = ((), (), s32[]{:S(2)}) async-start(), calls=%async_computation.10 | async-start | bytes 2097152 | tf_op jit(solution)/shard_map/psum | solution.py:9
  388.4 78.8 %all-gather.11.cloned.1.call-start = ((), (), s32[]{:S(2)}) async-start(), calls=%async_computation.11 | async-start | bytes 1179648 | tf_op jit(solution)/shard_map/all_gather | solution.py:37
Sparse Core Ops, SparseCore 0:
  22.2 71.0 reduce-scatter.1
  95.4 39.2 all-gather.4
  166.9 35.1 all-reduce.3
  204.8 40.7 all-gather.6
  277.7 35.1 all-reduce.5
  315.6 40.7 all-gather.8
  388.6 35.1 all-reduce.7
  426.5 40.7 all-gather.10
